TPU v7x, 32 devices: a whole 2x2x4 slice. The times are simulated.
32 devices in a mesh: dp: 2 (over x), tp: 16 (over z, y, core).
Axes of the slice: x: 2, y: 2, z: 4, core: 2. Of those that a mesh axis runs over, the one named last changes fastest.
Arguments:
- hidden: bfloat16 [512, 2304], P('dp', 'tp'), parts along dimension 0
- cand_ids: int32 [512, 4], P('dp'), parts along dimension 0
- norm_scale: bfloat16 [2304], P('tp')
- emb_table: bfloat16 [256000, 2304], P('tp')
Outputs:
- output 1: float32 [512], P('dp'), parts along dimension 0
- output 2: float32 [512, 4], P('dp'), parts along dimension 0
- output 3: bfloat16 [512, 256000], P('dp', 'tp'), parts along dimension 0
There are 2 independent parts. A program takes and returns all parts, laid end to end along the dimension named above; an argument that names none is the same for every part.
All inputs are finite; a program needn't handle non-finite values.
Results may differ from a plain program's by a relative error of at most 0.001.
Values are sent between devices in bfloat16 or wider.
A program may use at most 1 GiB of HBM per device.

v0:
```python
import jax
import jax.numpy as jnp
from jax import lax
from jax.sharding import PartitionSpec as P

NORM_EPS = 1e-6
SOFT_CAP = 30.0


def solution(mesh):
    group_size = mesh.shape["tp"]

    def device_step(hidden_blk, cand_ids, scale_blk, table_blk):
        hidden_f32 = hidden_blk.astype(jnp.float32)
        full_width = hidden_blk.shape[1] * group_size
        sq_sum = lax.psum(jnp.sum(hidden_f32 * hidden_f32, axis=1, keepdims=True), "tp")
        normed = (hidden_f32 * lax.rsqrt(sq_sum / full_width + NORM_EPS) * (1.0 + scale_blk.astype(jnp.float32))).astype(jnp.bfloat16)
        full_normed = lax.all_gather(normed, "tp", axis=1, tiled=True)
        logits = lax.dot_general(full_normed, table_blk, (((1,), (1,)), ((), ())), preferred_element_type=jnp.float32)
        capped = SOFT_CAP * jnp.tanh(logits / SOFT_CAP)
        local_max = jnp.max(capped, axis=1)
        local_sum = jnp.sum(jnp.exp(capped - local_max[:, None]), axis=1)
        shard_stats = lax.all_gather(jnp.stack([local_max, local_sum]), "tp")
        glob_max = jnp.max(shard_stats[:, 0], axis=0)
        glob_sum = jnp.sum(shard_stats[:, 1] * jnp.exp(shard_stats[:, 0] - glob_max[None, :]), axis=0)
        row_lse = glob_max + jnp.log(glob_sum)
        log_probs = capped - row_lse[:, None]
        vocab_local = table_blk.shape[0]
        local_ids = cand_ids - lax.axis_index("tp") * vocab_local
        is_owned = (local_ids >= 0) & (local_ids < vocab_local)
        picked = jnp.take_along_axis(capped, jnp.clip(local_ids, 0, vocab_local - 1), axis=1)
        cand_capped = lax.psum(jnp.where(is_owned, picked, 0.0), "tp")
        return row_lse, cand_capped - row_lse[:, None], log_probs.astype(jnp.bfloat16)

    return jax.shard_map(
        device_step,
        mesh=mesh,
        in_specs=(P("dp", "tp"), P("dp", None), P("tp"), P("tp", None)),
        out_specs=(P("dp"), P("dp", None), P("dp", "tp")),
        check_vma=False,
    )
```

profile of v0, /device:TPU:0, one launch (start us, length us, event | category | flops | bytes accessed | tf_op | source)
XLA Modules:
  0.0 212.6 jit_solution(7725743221175600803)
XLA Ops:
  7.2 0.0 all-gather.4.cloned.1.call-start
  7.2 0.9 fusion.2
  8.1 35.0 %psum.14 = f32[256,1]{0,1:T(1,128)S(1)} all-reduce(f32[256,1]{0,1:T(1,128)S(1)} %bitcast.25), channel_id=1, replica_groups=mesh['dp'=2,'tp'=16] {'tp'}, use_global_device_ids=true, to_apply=%region_1.0 | all-reduce | flops 256 | bytes 2048 | tf_op jit(solution)/shard_map/psum | solution.py:16
  43.1 0.7 convert_add_fusion
  43.8 1.6 fusion.4
  45.4 0.0 all-gather.4.cloned.1.call-update
  45.4 0.7 bitcast_or_fusion
  46.1 0.1 copy.25
  46.3 0.1 reshape.25
  46.4 34.8 %all-gather.4.cloned.1.call-done = bf16[256,2304]{0,1:T(8,128)(2,1)} async-done(((bf16[256,144]{0,1:T(8,128)(2,1)}), bf16[256,2304]{0,1:T(8,128)(2,1)}) %all-gather.4.cloned.1.call-update) | async-done | bytes 1179664 | tf_op jit(solution)/shard_map/all_gather | solution.py:18
  81.2 34.1 %fusion.9 = (f32[256]{0:T(256)S(1)}, f32[256,16000]{1,0:T(8,128)}) fusion(bf16[256,2304]{0,1:T(8,128)(2,1)} %all-gather.4.cloned.1.call-done, bf16[16000,2304]{1,0:T(8,128)(2,1)} %param.7), kind=kOutput, calls=%fused_computation.26 | convolution fusion | flops 18886656000 | bytes 91292672 | tf_op jit(solution)/shard_map/dot_general | solution.py:19
  115.3 8.0 %exponential_reduce_fusion = f32[256]{0:T(256)S(1)} fusion(f32[256,16000]{1,0:T(8,128)} %get-tuple-element.13, f32[256]{0:T(256)S(1)} %get-tuple-element.12), kind=kLoop, calls=%fused_computation.5 | loop fusion | flops 8191744 | bytes 16386048 | tf_op jit(solution)/shard_map/reduce_sum | solution.py:22
  123.3 19.4 %all-gather.1 = f32[16,2,256]{2,1,0:T(2,128)S(1)} all-gather(f32[1,2,256]{2,1,0:T(2,128)S(1)} %maximum_bitcast_fusion), channel_id=2, replica_groups=mesh['dp'=2,'tp'=16] {'tp'}, dimensions={0}, use_global_device_ids=true | all-gather | bytes 34816 | tf_op jit(solution)/shard_map/all_gather | solution.py:23
  142.8 0.0 copy-start.1
  142.8 0.0 copy-start
  142.8 23.6 %gather_fusion = f32[1024]{0:T(1024)S(1)} fusion(f32[256,16000]{1,0:T(8,128)} %get-tuple-element.13, s32[1024]{0:T(1024)S(1)} %reshape.25), kind=kCustom, calls=%fused_computation | custom fusion | bytes 16384 | tf_op jit(solution)/shard_map/jit(take_along_axis)/gather | solution.py:31
  166.5 0.1 reshape.28
  166.6 0.1 copy.26
  166.7 0.0 copy-done
  166.7 29.5 %psum.15 = f32[256,4]{0,1:T(4,128)S(1)} all-reduce(f32[256,4]{0,1:T(4,128)S(1)} %select_select_fusion), channel_id=1, replica_groups=mesh['dp'=2,'tp'=16] {'tp'}, use_global_device_ids=true, to_apply=%region_6.7 | all-reduce | flops 1024 | bytes 8192 | tf_op jit(solution)/shard_map/psum | solution.py:32
  196.2 8.9 %subtract_convert_fusion = bf16[256,16000]{1,0:T(8,128)(2,1)} fusion(f32[256,16000]{1,0:T(8,128)} %get-tuple-element.13, f32[256]{0:T(256)S(1)} %log_add_fusion), kind=kLoop, calls=%fused_computation.4 | loop fusion | flops 8192000 | bytes 24577024 | tf_op jit(solution)/shard_map/convert_element_type | solution.py:33
  205.1 0.0 copy-done.1
  205.1 0.6 broadcast_subtract_fusion
  (6 shorter events, 0.1 us)
Async XLA Ops:
  7.2 74.0 %all-gather.4.cloned.1.call-start = ((), (), s32[]{:S(2)}) async-start(), calls=%async_computation | async-start | bytes 1253376 | tf_op jit(solution)/shard_map/all_gather | solution.py:18
  142.8 62.3 %copy-start.1 = (f32[256]{0:T(256)}, f32[256]{0:T(256)S(1)}, u32[]{:S(2)}) copy-start(f32[256]{0:T(256)S(1)} %log_add_fusion) | copy-start | bytes 3076
  142.8 23.9 %copy-start = (s32[256,4]{0,1:T(4,128)S(1)}, s32[256,4]{0,1:T(4,128)}, u32[]{:S(2)}) copy-start(s32[256,4]{0,1:T(4,128)} %param.5) | copy-start | bytes 12292
Sparse Core Ops, SparseCore 0:
  45.5 35.6 all-gather.3
where the time goes:
time: 214 us; the launch traced here: 213 us
  blocking collectives  83.9 us (39%)
  waiting for transfers between devices  34.8 us (16%)
  matrix products  34.1 us (16%)
  local copies, waits for them, and re-layouts  24.1 us (11%)
  other arithmetic  21.5 us (10%)
  between operations  14.1 us (7%)
    psum x1, blocking collectives, device_step(): lax.psum(jnp.sum(hidden_f32 * hidden_f32, axis=1, keepdims=True), 'tp')  35 us
    all_gather x1, waiting for transfers between devices, device_step(): full_normed = lax.all_gather(normed, 'tp', axis=1, tiled=True)  34.8 us
    dot_general x1, matrix products, device_step(): lax.dot_general(full_normed, table_blk, (((1,), (1,)), ((), ())), preferr...  34.1 us
    psum x1, blocking collectives, device_step(): cand_capped = lax.psum(jnp.where(is_owned, picked, 0.0), 'tp')  29.5 us
    gather x5, local copies, waits for them, and re-layouts, device_step(): jnp.take_along_axis(capped, jnp.clip(local_ids, 0, vocab_local - 1), axis=1)  24.1 us
    all_gather x1, blocking collectives, device_step(): shard_stats = lax.all_gather(jnp.stack([local_max, local_sum]), 'tp')  19.4 us
    convert_element_type x1, other arithmetic, device_step(): log_probs.astype(jnp.bfloat16)  8.88 us
    reduce_sum x1, other arithmetic, device_step(): local_sum = jnp.sum(jnp.exp(capped - local_max[:, None]), axis=1)  7.98 us
  transfers between devices with their start and end apart: 1, of which 1 were waited for; matrix products, arithmetic and copies ran while one was open for 0% of the time, Pallas kernels for 0%

commit v1 on v0

v1 whole, which is shorter than its diff:
```python
import functools

import jax
import jax.numpy as jnp
from jax import lax
from jax.experimental import pallas as pl
from jax.experimental.pallas import tpu as pltpu
from jax.sharding import PartitionSpec as P

NORM_EPS = 1e-6
SOFT_CAP = 30.0
MESH = pl.DeviceIdType.MESH
CORES, YS = 2, 2

TILE = 1600
SLOTS = 5
PIECE = 160
GROUP = 16
OUT_TILE = 3200


def stream_kernel(
    n_dev, n_feat, hid_ref, scale_ref, ids_ref, table_ref, capped_ref, lse_ref, cand_ref,
    ring, za, zb, rows, scales, normed, ids8, stats,
    ring_sem, own_sem, row_send, row_recv, scale_send, scale_recv, stat_send, stat_recv,
):
    d_loc, batch = hid_ref.shape
    vocab = table_ref.shape[0]
    tile = ring.shape[1]
    n_slots = ring.shape[0]
    n_tiles = vocab // tile
    piece = min(PIECE, tile // 2)
    n_cand = ids_ref.shape[0]

    me = lax.axis_index("tp")
    core = lax.rem(me, CORES)
    y = lax.rem(me // CORES, YS)
    z = me // (CORES * YS)
    n_z = n_dev // (CORES * YS)

    def index(z_, y_, c_):
        return (z_ * YS + y_) * CORES + c_

    def table_copy(b):
        slot = lax.rem(b, n_slots)
        return pltpu.make_async_copy(table_ref.at[pl.ds(b * tile, tile), :], ring.at[slot], ring_sem.at[slot])

    own_copy = pltpu.make_async_copy(hid_ref, rows.at[me], own_sem.at[0])
    own_copy.start()
    own_scale = pltpu.make_async_copy(scale_ref, scales.at[me], own_sem.at[1])
    own_scale.start()
    for b in range(n_slots):
        table_copy(b).start()

    barrier = pltpu.get_barrier_semaphore()
    for step in range(1, n_dev):
        pl.semaphore_signal(barrier, inc=1, device_id={"tp": lax.rem(me + step, n_dev)}, device_id_type=MESH)
    pl.semaphore_wait(barrier, n_dev - 1)

    own_copy.wait()
    own_scale.wait()

    def row_copy(slab, to, sem):
        return pltpu.make_async_remote_copy(
            src_ref=rows.at[slab], dst_ref=rows.at[slab], send_sem=row_send.at[sem], recv_sem=row_recv.at[slab],
            device_id={"tp": to}, device_id_type=MESH)

    def scale_copy(slab, to, sem):
        return pltpu.make_async_remote_copy(
            src_ref=scales.at[slab], dst_ref=scales.at[slab], send_sem=scale_send.at[sem], recv_sem=scale_recv.at[slab],
            device_id={"tp": to}, device_id_type=MESH)

    sibling = index(z, y, 1 - core)
    across = index(z, 1 - y, core)
    far_z = [z + 1 - 2 * lax.rem(z, 2), z + 2 - 4 * (z // 2), 3 - z] if n_z == 4 else [1 - z]
    sends = []

    def send(slab, to):
        copy = row_copy(slab, to, len(sends))
        copy.start()
        sends.append(copy)

    def arrive(slab):
        row_copy(slab, me, 0).wait_recv()

    send(me, across)
    for z_ in far_z:
        send(me, index(z_, y, core))
    send(me, sibling)
    scale_sends = []
    for step in range(1, n_dev):
        copy = scale_copy(me, lax.rem(me + step, n_dev), step - 1)
        copy.start()
        scale_sends.append(copy)

    for k in range(n_cand):
        ids8[8 * k:8 * k + 8, :] = jnp.broadcast_to(ids_ref[k:k + 1, :] - me * vocab, (8, batch))

    def squares(slab):
        f32 = rows[slab].astype(jnp.float32)
        return jnp.sum(f32 * f32, axis=0, keepdims=True)

    total = squares(me)
    for z_ in [z] + far_z:
        if z_ is not z:
            slab = index(z_, y, core)
            arrive(slab)
            send(slab, across)
            send(slab, sibling)
            total += squares(slab)
        slab = index(z_, 1 - y, core)
        arrive(slab)
        send(slab, sibling)
        total += squares(slab)
        for y_ in (y, 1 - y):
            slab = index(z_, y_, 1 - core)
            arrive(slab)
            total += squares(slab)
    for step in range(1, n_dev):
        scale_copy(lax.rem(me + step, n_dev), me, 0).wait_recv()

    inv = lax.rsqrt(total * (1.0 / n_feat) + NORM_EPS)
    wide = scales.shape[2]
    pad = [scales[d] for d in range(n_dev)] + [jnp.zeros((128 - n_dev, wide), jnp.float32)]
    scale_cols = jnp.concatenate(pad, axis=0).T
    for d in range(n_dev):
        gain = 1.0 + scale_cols[:d_loc, d:d + 1]
        normed[d * d_loc:(d + 1) * d_loc, :] = (rows[d].astype(jnp.float32) * inv * gain).astype(jnp.bfloat16)

    def tile_step(b, slot, dst, src, row0, carry):
        weights = normed[...]
        sums, picks = carry[0], list(carry[1:])
        for h in range(tile // piece):
            if dst is not None:
                dst[h * piece:(h + 1) * piece, :] = jnp.dot(
                    ring[slot, h * piece:(h + 1) * piece, :], weights, preferred_element_type=jnp.float32)
            for g in range(h * piece, (h + 1) * piece, GROUP):
                capped = jnp.tanh(src[g:g + GROUP, :] * (1.0 / SOFT_CAP)) * SOFT_CAP
                capped_ref[pl.ds(pl.multiple_of(row0 + g, 8), GROUP), :] = capped
                expd = jnp.exp(capped)
                for q in range(0, GROUP, 8):
                    sums = sums + expd[q:q + 8]
                    token = lax.broadcasted_iota(jnp.int32, (8, batch), 0) + (row0 + g + q)
                    for k in range(n_cand):
                        picks[k] = jnp.where(token == ids8[8 * k:8 * k + 8, :], capped[q:q + 8], picks[k])
        return (sums, *picks)

    zero = jnp.zeros((8, batch), jnp.float32)

    def pair(i, carry):
        b = 2 * i
        table_copy(b).wait()
        table_copy(b + 1).wait()
        for b_ in (b - 2, b - 1):
            @pl.when((b_ >= 0) & (b_ + n_slots < n_tiles))
            def _():
                table_copy(b_ + n_slots).start()
        first = jnp.where(i == 0, 0.0, 1.0)
        carry = tile_step(b, lax.rem(b, n_slots), za, zb, jnp.maximum(b - 1, 0) * tile, carry)
        carry = tuple(first * c for c in carry)
        return tile_step(b + 1, lax.rem(b + 1, n_slots), zb, za, b * tile, carry)

    zb[...] = jnp.zeros_like(zb)
    carry = lax.fori_loop(0, n_tiles // 2, pair, (zero,) * (1 + n_cand))
    carry = tile_step(None, None, None, zb, (n_tiles - 1) * tile, carry)

    mine = [jnp.sum(c, axis=0, keepdims=True) for c in carry]
    stats[me] = jnp.concatenate(mine + [jnp.zeros((7 - n_cand, batch), jnp.float32)], axis=0)

    def stat_copy(slab, to, sem):
        return pltpu.make_async_remote_copy(
            src_ref=stats.at[slab], dst_ref=stats.at[slab], send_sem=stat_send.at[sem], recv_sem=stat_recv.at[slab],
            device_id={"tp": to}, device_id_type=MESH)

    stat_sends = []
    for step in range(1, n_dev):
        copy = stat_copy(me, lax.rem(me + step, n_dev), step - 1)
        copy.start()
        stat_sends.append(copy)
    for copy in sends + scale_sends:
        copy.wait_send()
    for step in range(1, n_dev):
        stat_copy(lax.rem(me + step, n_dev), me, 0).wait_recv()
    joined = stats[0]
    for d in range(1, n_dev):
        joined += stats[d]
    lse = jnp.log(joined[0:1, :])
    lse_ref[...] = lse
    cand_ref[...] = joined[1:1 + n_cand, :] - lse
    for copy in stat_sends:
        copy.wait_send()


def finish_kernel(capped_ref, lse_in, cand_in, out_ref, lse_ref, cand_ref, held, sem):
    tokens = held.shape[2]
    copies = []
    for i in range(held.shape[0]):
        part = (capped_ref[i * tokens:(i + 1) * tokens, :] - lse_in[...]).astype(jnp.bfloat16)
        held[i] = part.T
        copy = pltpu.make_async_copy(held.at[i], out_ref.at[:, pl.ds(i * tokens, tokens)], sem.at[i])
        copy.start()
        copies.append(copy)
    lse_ref[...] = lse_in[...]
    cand_ref[...] = cand_in[...]
    for copy in copies:
        copy.wait()


def solution(mesh):
    n_dev = mesh.shape["tp"]

    def device_step(hidden_blk, cand_ids, scale_blk, table_blk):
        batch, d_loc = hidden_blk.shape
        vocab, n_feat = table_blk.shape
        n_cand = cand_ids.shape[1]
        tile = min(TILE, vocab // 2)
        wide = -(-d_loc // 128) * 128
        scale_row = jnp.pad(scale_blk.astype(jnp.float32)[None, :], ((0, 0), (0, wide - d_loc)))
        any_spec = pl.BlockSpec(memory_space=pl.ANY)
        vmem_spec = pl.BlockSpec(memory_space=pltpu.VMEM)
        dma = pltpu.SemaphoreType.DMA
        capped, lse, cand = pl.pallas_call(
            functools.partial(stream_kernel, n_dev, n_feat),
            out_shape=[
                pltpu.VMEM((vocab, batch), jnp.float32),
                pltpu.VMEM((1, batch), jnp.float32),
                pltpu.VMEM((n_cand, batch), jnp.float32),
            ],
            in_specs=[any_spec, any_spec, vmem_spec, any_spec],
            out_specs=[vmem_spec, vmem_spec, vmem_spec],
            scratch_shapes=[
                pltpu.VMEM((min(SLOTS, vocab // tile), tile, n_feat), jnp.bfloat16),
                pltpu.VMEM((tile, batch), jnp.float32),
                pltpu.VMEM((tile, batch), jnp.float32),
                pltpu.VMEM((n_dev, d_loc, batch), jnp.bfloat16),
                pltpu.VMEM((n_dev, 1, wide), jnp.float32),
                pltpu.VMEM((n_feat, batch), jnp.bfloat16),
                pltpu.VMEM((8 * n_cand, batch), jnp.int32),
                pltpu.VMEM((n_dev, 8, batch), jnp.float32),
                dma((min(SLOTS, vocab // tile),)),
                dma((2,)),
                dma((n_dev,)),
                dma((n_dev,)),
                dma((n_dev,)),
                dma((n_dev,)),
                dma((n_dev,)),
                dma((n_dev,)),
            ],
            compiler_params=pltpu.CompilerParams(
                collective_id=0, has_side_effects=True, vmem_limit_bytes=46 * 1024 * 1024),
            cost_estimate=pl.CostEstimate(
                flops=2 * batch * vocab * n_feat, bytes_accessed=2 * vocab * n_feat, transcendentals=2 * batch * vocab),
            name="stream",
        )(hidden_blk.T, scale_row, cand_ids.T, table_blk)
        out_tile = min(OUT_TILE, vocab // 2)
        log_probs, lse, cand = pl.pallas_call(
            finish_kernel,
            out_shape=[
                jax.ShapeDtypeStruct((batch, vocab), jnp.bfloat16),
                jax.ShapeDtypeStruct((1, batch), jnp.float32),
                jax.ShapeDtypeStruct((n_cand, batch), jnp.float32),
            ],
            in_specs=[vmem_spec, vmem_spec, vmem_spec],
            out_specs=[any_spec, vmem_spec, vmem_spec],
            scratch_shapes=[
                pltpu.VMEM((vocab // out_tile, batch, out_tile), jnp.bfloat16),
                dma((vocab // out_tile,)),
            ],
            compiler_params=pltpu.CompilerParams(vmem_limit_bytes=24 * 1024 * 1024),
            name="finish",
        )(capped, lse, cand)
        return lse.reshape(batch), cand.T, log_probs

    return jax.shard_map(
        device_step,
        mesh=mesh,
        in_specs=(P("dp", "tp"), P("dp", None), P("tp"), P("tp", None)),
        out_specs=(P("dp"), P("dp", None), P("dp", "tp")),
        check_vma=False,
    )
```

time: 214 us -> 67.1 us (0.31)
  blocking collectives: 83.9 us -> 0 us
  Pallas kernels: 0 us -> 65 us
  waiting for transfers between devices: 34.8 us -> 0 us
  matrix products: 34.1 us -> 0 us
  local copies, waits for them, and re-layouts: 24.1 us -> 0.66 us
  other arithmetic: 21.5 us -> 0.57 us
  between operations: 14.1 us -> 0.64 us
    pallas_call x0 -> x2, Pallas kernels: none -> 65 us  [the longest x1 60.6 us: device_step(): pl.pallas_call(functools.partial(stream_kernel, n_dev, n_feat), out_shape...]
    psum x2 -> x0, blocking collectives: 64.5 us -> none  [the longest x1 35 us: device_step(): lax.psum(jnp.sum(hidden_f32 * hidden_f32, axis=1, keepdims=True), 'tp')]
    all_gather x1 -> x0, waiting for transfers between devices: 34.8 us -> none  [device_step(): full_normed = lax.all_gather(normed, 'tp', axis=1, tiled=True)]
    dot_general x1 -> x0, matrix products: 34.1 us -> none  [device_step(): lax.dot_general(full_normed, table_blk, (((1,), (1,)), ((), ())), preferr...]
    gather x5 -> x0, local copies, waits for them, and re-layouts: 24.1 us -> none  [device_step(): jnp.take_along_axis(capped, jnp.clip(local_ids, 0, vocab_local - 1), axis=1)]
    all_gather x1 -> x0, blocking collectives: 19.4 us -> none  [device_step(): shard_stats = lax.all_gather(jnp.stack([local_max, local_sum]), 'tp')]
    convert_element_type x2 -> x0, other arithmetic: 10.5 us -> none  [the longest x1 8.88 us: device_step(): log_probs.astype(jnp.bfloat16)]
    reduce_sum x3 -> x0, other arithmetic: 8.92 us -> none  [the longest x1 7.98 us: device_step(): local_sum = jnp.sum(jnp.exp(capped - local_max[:, None]), axis=1)]
  transfers between devices with their start and end apart: 1 -> 0, of which waited for: 1 -> 0; matrix products, arithmetic and copies ran while one was open for 0% -> 0% of each run, Pallas kernels for 0% -> 0%
where the time goes in v1:
time: 67.1 us; the launch traced here: 66.9 us
  Pallas kernels  65 us (97%)
    pallas_call x1, Pallas kernels, device_step(): pl.pallas_call(functools.partial(stream_kernel, n_dev, n_feat), out_shape...  60.6 us
    pallas_call x1, Pallas kernels, device_step(): pl.pallas_call(finish_kernel, out_shape=[jax.ShapeDtypeStruct((batch, voc...  4.39 us

profile of v1, /device:TPU:0, one launch (start us, length us, event | category | flops | bytes accessed | tf_op | source)
XLA Modules:
  0.0 66.9 jit_solution(13543512480848484581)
XLA Ops:
  0.6 0.7 broadcast_in_dim.4
  1.3 0.6 pad_convert_fusion.scale_ref
  1.9 60.6 %stream.1 = (f32[16000,256]{1,0:T(8,128)S(1)}, f32[1,256]{1,0:T(1,128)S(1)}, f32[4,256]{1,0:T(4,128)S(1)}) custom-call(bf16[144,256]{1,0:T(8,128)(2,1)} %bitcast.4, f32[1,256]{1,0:T(1,128)} %pad_convert_fusion.scale_ref, s32[4,256]{1,0:T(4,128)} %bitcast.5, bf16[16000,2304]{1,0:T(8,128)(2,1)} %table_ref.1), custom_call_target="tpu_custom_call" | custom-call | flops 18874368000 | bytes 73728000 | tf_op jit(solution)/shard_map/stream/pallas_call | solution.py:222
  62.5 4.4 %finish.1 = (bf16[256,16000]{1,0:T(8,128)(2,1)}, f32[1,256]{1,0:T(1,128)}, f32[4,256]{1,0:T(4,128)}) custom-call(f32[16000,256]{1,0:T(8,128)S(1)} %get-tuple-element.9.capped_ref, f32[1,256]{1,0:T(1,128)S(1)} %get-tuple-element.10.lse_in, f32[4,256]{1,0:T(4,128)S(1)} %get-tuple-element.11.cand_in), custom_call_target="tpu_custom_call" | custom-call | tf_op jit(solution)/shard_map/finish/pallas_call | solution.py:256

commit v2 on v1

v2 whole, which is shorter than its diff:
```python
import functools

import jax
import jax.numpy as jnp
from jax import lax
from jax.experimental import pallas as pl
from jax.experimental.pallas import tpu as pltpu
from jax.sharding import PartitionSpec as P

NORM_EPS = 1e-6
SOFT_CAP = 30.0
MESH = pl.DeviceIdType.MESH
CORES, YS = 2, 2

TILE = 1600
SLOTS = 5
PIECE = 160
GROUP = 16
OUT_UNIT = 640
PARTS = 3


def stream_kernel(
    n_dev, n_feat, hid_ref, scale_ref, ids_ref, table_ref, capped_ref, lse_ref, cand_ref,
    ring, za, zb, rows, scales, normed, ids8, stats,
    ring_sem, own_sem, row_send, row_recv, scale_send, scale_recv, stat_send, stat_recv,
):
    d_loc, batch = hid_ref.shape
    vocab = table_ref.shape[0]
    n_slots, tile, _ = ring.shape
    n_tiles = vocab // tile
    piece = min(PIECE, tile // 2)
    n_cand = ids_ref.shape[0]
    parts = row_recv.shape[1]
    part = d_loc // parts

    me = lax.axis_index("tp")
    core = lax.rem(me, CORES)
    y = lax.rem(me // CORES, YS)
    z = me // (CORES * YS)

    def index(z_, y_, c_):
        return (z_ * YS + y_) * CORES + c_

    def table_copy(b):
        slot = lax.rem(b, n_slots)
        return pltpu.make_async_copy(table_ref.at[pl.ds(b * tile, tile), :], ring.at[slot], ring_sem.at[slot])

    own_copy = pltpu.make_async_copy(hid_ref, rows.at[me], own_sem.at[0])
    own_copy.start()
    for b in range(n_slots):
        table_copy(b).start()

    barrier = pltpu.get_barrier_semaphore()
    for step in range(1, n_dev):
        pl.semaphore_signal(barrier, inc=1, device_id={"tp": lax.rem(me + step, n_dev)}, device_id_type=MESH)

    wide = scales.shape[2]
    scale_row = scale_ref[...].astype(jnp.float32)
    scales[me] = jnp.concatenate([scale_row, jnp.zeros((1, wide - d_loc), jnp.float32)], axis=1)
    for k in range(n_cand):
        ids8[8 * k:8 * k + 8, :] = jnp.broadcast_to(ids_ref[k:k + 1, :] - me * vocab, (8, batch))

    own_copy.wait()
    pl.semaphore_wait(barrier, n_dev - 1)

    sends = []

    def row_copy(slab, p, to, sem):
        where = rows.at[slab, p * part:(p + 1) * part, :]
        return pltpu.make_async_remote_copy(
            src_ref=where, dst_ref=where, send_sem=row_send.at[sem, p], recv_sem=row_recv.at[slab, p],
            device_id={"tp": to}, device_id_type=MESH)

    def send(k, slab, p, to):
        copy = row_copy(slab, p, to, k)
        copy.start()
        sends.append(copy)

    def arrive(slab, p):
        row_copy(slab, p, me, 0).wait_recv()

    def scale_copy(slab, to, sem):
        return pltpu.make_async_remote_copy(
            src_ref=scales.at[slab], dst_ref=scales.at[slab], send_sem=scale_send.at[sem], recv_sem=scale_recv.at[slab],
            device_id={"tp": to}, device_id_type=MESH)

    def squares(slab):
        f32 = rows[slab].astype(jnp.float32)
        return jnp.sum(f32 * f32, axis=0, keepdims=True)

    sibling = index(z, y, 1 - core)
    across = index(z, 1 - y, core)
    far_z = [z + 1 - 2 * lax.rem(z, 2), z + 2 - 4 * (z // 2), 3 - z]

    for p in range(parts):
        send(0, me, p, across)
        send(1, me, p, sibling)
    for j, z_ in enumerate(far_z):
        for p in range(parts):
            send(2 + j, me, p, index(z_, y, core))
    for step in range(1, n_dev):
        copy = scale_copy(me, lax.rem(me + step, n_dev), step - 1)
        copy.start()
        sends.append(copy)

    total = squares(me)

    def take_across(k, z_):
        slab = index(z_, 1 - y, core)
        for p in range(parts):
            arrive(slab, p)
            send(k, slab, p, sibling)
        return squares(slab)

    def take_column(k, z_):
        slab = index(z_, y, core)
        for p in range(parts):
            arrive(slab, p)
            send(k, slab, p, across)
            send(k + 1, slab, p, sibling)
        return squares(slab)

    total += take_across(5, z)
    total += take_column(6, far_z[0])
    total += take_column(8, far_z[1])
    total += take_across(12, far_z[0])
    total += take_column(10, far_z[2])
    total += take_across(13, far_z[1])
    total += take_across(14, far_z[2])
    for step in range(1, n_dev):
        scale_copy(lax.rem(me + step, n_dev), me, 0).wait_recv()
    pad = [scales[d] for d in range(n_dev)] + [jnp.zeros((128 - n_dev, wide), jnp.float32)]
    scale_cols = jnp.concatenate(pad, axis=0).T
    for z_ in [z] + far_z:
        for y_ in (y, 1 - y):
            slab = index(z_, y_, 1 - core)
            for p in range(parts):
                arrive(slab, p)
            total += squares(slab)

    inv = lax.rsqrt(total * (1.0 / n_feat) + NORM_EPS)
    for d in range(n_dev):
        gain = 1.0 + scale_cols[:d_loc, d:d + 1]
        normed[d * d_loc:(d + 1) * d_loc, :] = (rows[d].astype(jnp.float32) * inv * gain).astype(jnp.bfloat16)

    def dot_piece(b, dst, h):
        at = pl.ds(pl.multiple_of(h * piece, 16), piece)
        dst[at, :] = jnp.dot(ring[lax.rem(b, n_slots), at, :], normed[...], preferred_element_type=jnp.float32)

    def epilogue(src, row0, h, carry):
        def group(g, carry):
            at = h * piece + g * GROUP
            sums, picks = carry[0], list(carry[1:])
            capped = jnp.tanh(src[pl.ds(pl.multiple_of(at, 8), GROUP), :] * (1.0 / SOFT_CAP)) * SOFT_CAP
            capped_ref[pl.ds(pl.multiple_of(row0 + at, 8), GROUP), :] = capped
            expd = jnp.exp(capped)
            for q in range(0, GROUP, 8):
                sums = sums + expd[q:q + 8]
                token = lax.broadcasted_iota(jnp.int32, (8, batch), 0) + (row0 + at + q)
                for k in range(n_cand):
                    picks[k] = jnp.where(token == ids8[8 * k:8 * k + 8, :], capped[q:q + 8], picks[k])
            return (sums, *picks)

        return lax.fori_loop(0, piece // GROUP, group, carry, unroll=True)

    def step(b, dst, src, carry):
        table_copy(b).wait()

        def body(h, carry):
            dot_piece(b, dst, h)
            return carry if src is None else epilogue(src, (b - 1) * tile, h, carry)

        carry = lax.fori_loop(0, tile // piece, body, carry, unroll=True)
        @pl.when(b + n_slots < n_tiles)
        def _():
            table_copy(b + n_slots).start()
        return carry

    carry = (jnp.zeros((8, batch), jnp.float32),) * (1 + n_cand)
    carry = step(0, za, None, carry)

    def pair(i, carry):
        carry = step(2 * i + 1, zb, za, carry)
        return step(2 * i + 2, za, zb, carry)

    carry = lax.fori_loop(0, n_tiles // 2 - 1, pair, carry)
    last = n_tiles - 1
    carry = step(last, zb, za, carry)
    carry = lax.fori_loop(0, tile // piece, lambda h, c: epilogue(zb, last * tile, h, c), carry, unroll=True)

    mine = [jnp.sum(c, axis=0, keepdims=True) for c in carry]
    stats[me] = jnp.concatenate(mine + [jnp.zeros((7 - n_cand, batch), jnp.float32)], axis=0)

    def stat_copy(slab, to, sem):
        return pltpu.make_async_remote_copy(
            src_ref=stats.at[slab], dst_ref=stats.at[slab], send_sem=stat_send.at[sem], recv_sem=stat_recv.at[slab],
            device_id={"tp": to}, device_id_type=MESH)

    stat_sends = []
    for step_ in range(1, n_dev):
        copy = stat_copy(me, lax.rem(me + step_, n_dev), step_ - 1)
        copy.start()
        stat_sends.append(copy)
    for copy in sends:
        copy.wait_send()
    for step_ in range(1, n_dev):
        d = lax.rem(me + step_, n_dev)
        stat_copy(d, me, 0).wait_recv()
    joined = stats[0]
    for d in range(1, n_dev):
        joined += stats[d]
    lse = jnp.log(joined[0:1, :])
    lse_ref[...] = lse
    cand_ref[...] = joined[1:1 + n_cand, :] - lse
    for copy in stat_sends:
        copy.wait_send()


def finish_kernel(capped_ref, lse_in, cand_in, out_ref, lse_ref, cand_ref, held, sem):
    small = [pltpu.make_async_copy(lse_in, lse_ref, sem.at[0]), pltpu.make_async_copy(cand_in, cand_ref, sem.at[1])]
    for copy in small:
        copy.start()
    copies = []
    start = 0
    for i, tokens in enumerate(pieces_of(held.shape[1])):
        part = (capped_ref[start:start + tokens, :] - lse_in[...]).astype(jnp.bfloat16)
        held[:, start:start + tokens] = part.T
        copy = pltpu.make_async_copy(
            held.at[:, pl.ds(start, tokens)], out_ref.at[:, pl.ds(start, tokens)], sem.at[2 + i])
        copy.start()
        copies.append(copy)
        start += tokens
    for copy in small + copies:
        copy.wait()


def pieces_of(tokens):
    left, out = tokens // OUT_UNIT, []
    for n in (1, 2, 4):
        if left > n + 7:
            out.append(n)
            left -= n
    while left > 6:
        out.append(4)
        left -= 4
    out += {0: [], 1: [1], 2: [1, 1], 3: [2, 1], 4: [3, 1], 5: [3, 1, 1], 6: [3, 2, 1]}[left]
    return [n * OUT_UNIT for n in out]


def solution(mesh):
    n_dev = mesh.shape["tp"]

    def device_step(hidden_blk, cand_ids, scale_blk, table_blk):
        batch, d_loc = hidden_blk.shape
        vocab, n_feat = table_blk.shape
        n_cand = cand_ids.shape[1]
        tile = min(TILE, vocab // 2)
        wide = -(-d_loc // 128) * 128
        parts = PARTS if d_loc % (16 * PARTS) == 0 else 1
        any_spec = pl.BlockSpec(memory_space=pl.ANY)
        vmem_spec = pl.BlockSpec(memory_space=pltpu.VMEM)
        dma = pltpu.SemaphoreType.DMA
        capped, lse, cand = pl.pallas_call(
            functools.partial(stream_kernel, n_dev, n_feat),
            out_shape=[
                pltpu.VMEM((vocab, batch), jnp.float32),
                pltpu.VMEM((1, batch), jnp.float32),
                pltpu.VMEM((n_cand, batch), jnp.float32),
            ],
            in_specs=[any_spec, vmem_spec, vmem_spec, any_spec],
            out_specs=[vmem_spec, vmem_spec, vmem_spec],
            scratch_shapes=[
                pltpu.VMEM((min(SLOTS, vocab // tile), tile, n_feat), jnp.bfloat16),
                pltpu.VMEM((tile, batch), jnp.float32),
                pltpu.VMEM((tile, batch), jnp.float32),
                pltpu.VMEM((n_dev, d_loc, batch), jnp.bfloat16),
                pltpu.VMEM((n_dev, 1, wide), jnp.float32),
                pltpu.VMEM((n_feat, batch), jnp.bfloat16),
                pltpu.VMEM((8 * n_cand, batch), jnp.int32),
                pltpu.VMEM((n_dev, 8, batch), jnp.float32),
                dma((min(SLOTS, vocab // tile),)),
                dma((1,)),
                dma((n_dev, parts)),
                dma((n_dev, parts)),
                dma((n_dev,)),
                dma((n_dev,)),
                dma((n_dev,)),
                dma((n_dev,)),
            ],
            compiler_params=pltpu.CompilerParams(
                collective_id=0, has_side_effects=True, vmem_limit_bytes=46 * 1024 * 1024),
            cost_estimate=pl.CostEstimate(
                flops=2 * batch * vocab * n_feat, bytes_accessed=2 * vocab * n_feat, transcendentals=2 * batch * vocab),
            name="stream",
        )(hidden_blk.T, scale_blk[None, :], cand_ids.T, table_blk)
        log_probs, lse, cand = pl.pallas_call(
            finish_kernel,
            out_shape=[
                jax.ShapeDtypeStruct((batch, vocab), jnp.bfloat16),
                jax.ShapeDtypeStruct((1, batch), jnp.float32),
                jax.ShapeDtypeStruct((n_cand, batch), jnp.float32),
            ],
            in_specs=[vmem_spec, vmem_spec, vmem_spec],
            out_specs=[any_spec, any_spec, any_spec],
            scratch_shapes=[
                pltpu.VMEM((batch, vocab), jnp.bfloat16),
                dma((2 + len(pieces_of(vocab)),)),
            ],
            compiler_params=pltpu.CompilerParams(vmem_limit_bytes=24 * 1024 * 1024),
            name="finish",
        )(capped, lse, cand)
        return lse.reshape(batch), cand.T, log_probs

    return jax.shard_map(
        device_step,
        mesh=mesh,
        in_specs=(P("dp", "tp"), P("dp", None), P("tp"), P("tp", None)),
        out_specs=(P("dp"), P("dp", None), P("dp", "tp")),
        check_vma=False,
    )
```

time: 67.1 us -> 59.5 us (0.89)
  Pallas kernels: 65 us -> 56.8 us
    pallas_call x1, Pallas kernels: 60.6 us -> 53.1 us  [device_step(): pl.pallas_call(functools.partial(stream_kernel, n_dev, n_feat), out_shape...]
    pallas_call x1, Pallas kernels: 4.39 us -> 3.65 us  [device_step(): pl.pallas_call(finish_kernel, out_shape=[jax.ShapeDtypeStruct((batch, voc...]
where the time goes in v2:
time: 59.5 us; the launch traced here: 58.8 us
  Pallas kernels  56.8 us (95%)
  local copies, waits for them, and re-layouts  1.22 us (2%)
  between operations  0.8 us (1%)
    pallas_call x1, Pallas kernels, device_step(): pl.pallas_call(functools.partial(stream_kernel, n_dev, n_feat), out_shape...  53.1 us
    pallas_call x1, Pallas kernels, device_step(): pl.pallas_call(finish_kernel, out_shape=[jax.ShapeDtypeStruct((batch, voc...  3.65 us
    broadcast_in_dim x1, local copies, waits for them, and re-layouts, device_step(): scale_blk[None, :]  1.22 us

profile of v2, /device:TPU:0, one launch (start us, length us, event | category | flops | bytes accessed | tf_op | source)
XLA Modules:
  0.0 58.8 jit_solution(3107208842972708769)
XLA Ops:
  0.6 1.2 %broadcast_in_dim.3.scale_ref = bf16[1,144]{1,0:T(2,128)(2,1)} reshape(bf16[144]{0:T(256)(128)(2,1)} %param.6) | data formatting | bytes 576 | tf_op jit(solution)/shard_map/broadcast_in_dim | solution.py:296
  1.9 53.1 %stream.1 = (f32[16000,256]{1,0:T(8,128)S(1)}, f32[1,256]{1,0:T(1,128)S(1)}, f32[4,256]{1,0:T(4,128)S(1)}) custom-call(bf16[144,256]{1,0:T(8,128)(2,1)} %bitcast.4, bf16[1,144]{1,0:T(2,128)(2,1)} %broadcast_in_dim.3.scale_ref, s32[4,256]{1,0:T(4,128)} %bitcast.5, bf16[16000,2304]{1,0:T(8,128)(2,1)} %table_ref.1), custom_call_target="tpu_custom_call" | custom-call | flops 18874368000 | bytes 73728000 | tf_op jit(solution)/shard_map/stream/pallas_call | solution.py:264
  55.0 3.7 %finish.1 = (bf16[256,16000]{1,0:T(8,128)(2,1)}, f32[1,256]{1,0:T(1,128)}, f32[4,256]{1,0:T(4,128)}) custom-call(f32[16000,256]{1,0:T(8,128)S(1)} %get-tuple-element.9.capped_ref, f32[1,256]{1,0:T(1,128)S(1)} %get-tuple-element.10.lse_in, f32[4,256]{1,0:T(4,128)S(1)} %get-tuple-element.11.cand_in), custom_call_target="tpu_custom_call" | custom-call | tf_op jit(solution)/shard_map/finish/pallas_call | solution.py:297

commit v3 on v2

--- a/solution.py
+++ b/solution.py
@@ -17,6 +17,7 @@
 PIECE = 160
 GROUP = 16
 OUT_UNIT = 640
+EARLY = 1
 PARTS = 3
 
 
@@ -48,7 +49,7 @@
 
     own_copy = pltpu.make_async_copy(hid_ref, rows.at[me], own_sem.at[0])
     own_copy.start()
-    for b in range(n_slots):
+    for b in range(EARLY):
         table_copy(b).start()
 
     barrier = pltpu.get_barrier_semaphore()
@@ -56,7 +57,7 @@
         pl.semaphore_signal(barrier, inc=1, device_id={"tp": lax.rem(me + step, n_dev)}, device_id_type=MESH)
 
     wide = scales.shape[2]
-    scale_row = scale_ref[...].astype(jnp.float32)
+    scale_row = scale_ref[...].astype(jnp.float32).reshape(1, d_loc)
     scales[me] = jnp.concatenate([scale_row, jnp.zeros((1, wide - d_loc), jnp.float32)], axis=1)
     for k in range(n_cand):
         ids8[8 * k:8 * k + 8, :] = jnp.broadcast_to(ids_ref[k:k + 1, :] - me * vocab, (8, batch))
@@ -128,6 +129,8 @@
     total += take_column(10, far_z[2])
     total += take_across(13, far_z[1])
     total += take_across(14, far_z[2])
+    for b in range(EARLY, n_slots):
+        table_copy(b).start()
     for step in range(1, n_dev):
         scale_copy(lax.rem(me + step, n_dev), me, 0).wait_recv()
     pad = [scales[d] for d in range(n_dev)] + [jnp.zeros((128 - n_dev, wide), jnp.float32)]
@@ -293,7 +296,7 @@
             cost_estimate=pl.CostEstimate(
                 flops=2 * batch * vocab * n_feat, bytes_accessed=2 * vocab * n_feat, transcendentals=2 * batch * vocab),
             name="stream",
-        )(hidden_blk.T, scale_blk[None, :], cand_ids.T, table_blk)
+        )(hidden_blk.T, scale_blk, cand_ids.T, table_blk)
         log_probs, lse, cand = pl.pallas_call(
             finish_kernel,
             out_shape=[

time: 59.5 us -> 52.3 us (0.88)
  Pallas kernels: 56.8 us -> 50.8 us
  local copies, waits for them, and re-layouts: 1.22 us -> 0 us
    pallas_call x1, Pallas kernels: 53.1 us -> 47.1 us  [device_step(): pl.pallas_call(functools.partial(stream_kernel, n_dev, n_feat), out_shape...]
    broadcast_in_dim x1 -> x0, local copies, waits for them, and re-layouts: 1.22 us -> none  [device_step(): scale_blk[None, :]]
where the time goes in v3:
time: 52.3 us; the launch traced here: 51.6 us
  Pallas kernels  50.8 us (97%)
  between operations  0.8 us (2%)
    pallas_call x1, Pallas kernels, device_step(): pl.pallas_call(functools.partial(stream_kernel, n_dev, n_feat), out_shape...  47.1 us
    pallas_call x1, Pallas kernels, device_step(): pl.pallas_call(finish_kernel, out_shape=[jax.ShapeDtypeStruct((batch, voc...  3.65 us

profile of v3, /device:TPU:0, one launch (start us, length us, event | category | flops | bytes accessed | tf_op | source)
XLA Modules:
  0.0 51.6 jit_solution(1425503315227334591)
XLA Ops:
  0.6 47.1 %stream.1 = (f32[16000,256]{1,0:T(8,128)S(1)}, f32[1,256]{1,0:T(1,128)S(1)}, f32[4,256]{1,0:T(4,128)S(1)}) custom-call(bf16[144,256]{1,0:T(8,128)(2,1)} %bitcast.4, bf16[144]{0:T(256)(128)(2,1)} %scale_ref.1, s32[4,256]{1,0:T(4,128)} %bitcast.5, bf16[16000,2304]{1,0:T(8,128)(2,1)} %table_ref.1), custom_call_target="tpu_custom_call" | custom-call | flops 18874368000 | bytes 73728000 | tf_op jit(solution)/shard_map/stream/pallas_call | solution.py:267
  47.7 3.7 %finish.1 = (bf16[256,16000]{1,0:T(8,128)(2,1)}, f32[1,256]{1,0:T(1,128)}, f32[4,256]{1,0:T(4,128)}) custom-call(f32[16000,256]{1,0:T(8,128)S(1)} %get-tuple-element.9.capped_ref, f32[1,256]{1,0:T(1,128)S(1)} %get-tuple-element.10.lse_in, f32[4,256]{1,0:T(4,128)S(1)} %get-tuple-element.11.cand_in), custom_call_target="tpu_custom_call" | custom-call | tf_op jit(solution)/shard_map/finish/pallas_call | solution.py:300

commit v4 on v3

--- a/solution.py
+++ b/solution.py
@@ -17,14 +17,14 @@
 PIECE = 160
 GROUP = 16
 OUT_UNIT = 640
-EARLY = 1
+EARLY = 2
 PARTS = 3
 
 
 def stream_kernel(
     n_dev, n_feat, hid_ref, scale_ref, ids_ref, table_ref, capped_ref, lse_ref, cand_ref,
-    ring, za, zb, rows, scales, normed, ids8, stats,
-    ring_sem, own_sem, row_send, row_recv, scale_send, scale_recv, stat_send, stat_recv,
+    ring, z0, z1, z2, z3, z4, z5, rows, early, normed, ids_wide, stats,
+    near_sem, ring_sem, own_sem, row_send, row_recv, early_send, early_recv, stat_send, stat_recv,
 ):
     d_loc, batch = hid_ref.shape
     vocab = table_ref.shape[0]
@@ -43,26 +43,44 @@
     def index(z_, y_, c_):
         return (z_ * YS + y_) * CORES + c_
 
+    near = z // (n_dev // (CORES * YS) // 2)
+    near_len = max(128, n_feat // 2 // 256 * 256)
+    far_len = n_feat - near_len
+    near_at = pl.ds(pl.multiple_of(near * far_len, 128), near_len)
+    far_at = pl.ds(pl.multiple_of((1 - near) * near_len, 128), far_len)
+
     def table_copy(b):
         slot = lax.rem(b, n_slots)
         return pltpu.make_async_copy(table_ref.at[pl.ds(b * tile, tile), :], ring.at[slot], ring_sem.at[slot])
 
+    def near_copy(b):
+        return pltpu.make_async_copy(
+            table_ref.at[pl.ds(b * tile, tile), near_at], ring.at[b, :, near_at], near_sem.at[b])
+
+    def far_copy(b):
+        return pltpu.make_async_copy(
+            table_ref.at[pl.ds(b * tile, tile), far_at], ring.at[b, :, far_at], ring_sem.at[b])
+
     own_copy = pltpu.make_async_copy(hid_ref, rows.at[me], own_sem.at[0])
     own_copy.start()
     for b in range(EARLY):
-        table_copy(b).start()
+        near_copy(b).start()
 
     barrier = pltpu.get_barrier_semaphore()
     for step in range(1, n_dev):
         pl.semaphore_signal(barrier, inc=1, device_id={"tp": lax.rem(me + step, n_dev)}, device_id_type=MESH)
 
-    wide = scales.shape[2]
+    def squares(slab):
+        f32 = rows[slab].astype(jnp.float32)
+        return jnp.sum(f32 * f32, axis=0, keepdims=True)
+
+    wide = early.shape[2] - batch
     scale_row = scale_ref[...].astype(jnp.float32).reshape(1, d_loc)
-    scales[me] = jnp.concatenate([scale_row, jnp.zeros((1, wide - d_loc), jnp.float32)], axis=1)
+    own_copy.wait()
+    early[me] = jnp.concatenate([squares(me), scale_row, jnp.zeros((1, wide - d_loc), jnp.float32)], axis=1)
     for k in range(n_cand):
-        ids8[8 * k:8 * k + 8, :] = jnp.broadcast_to(ids_ref[k:k + 1, :] - me * vocab, (8, batch))
-
-    own_copy.wait()
+        ids_wide[GROUP * k:GROUP * (k + 1), :] = jnp.broadcast_to(ids_ref[k:k + 1, :] - me * vocab, (GROUP, batch))
+
     pl.semaphore_wait(barrier, n_dev - 1)
 
     sends = []
@@ -81,38 +99,31 @@
     def arrive(slab, p):
         row_copy(slab, p, me, 0).wait_recv()
 
-    def scale_copy(slab, to, sem):
+    def early_copy(slab, to, sem):
         return pltpu.make_async_remote_copy(
-            src_ref=scales.at[slab], dst_ref=scales.at[slab], send_sem=scale_send.at[sem], recv_sem=scale_recv.at[slab],
+            src_ref=early.at[slab], dst_ref=early.at[slab], send_sem=early_send.at[sem], recv_sem=early_recv.at[slab],
             device_id={"tp": to}, device_id_type=MESH)
-
-    def squares(slab):
-        f32 = rows[slab].astype(jnp.float32)
-        return jnp.sum(f32 * f32, axis=0, keepdims=True)
 
     sibling = index(z, y, 1 - core)
     across = index(z, 1 - y, core)
     far_z = [z + 1 - 2 * lax.rem(z, 2), z + 2 - 4 * (z // 2), 3 - z]
 
+    for step in range(1, n_dev):
+        copy = early_copy(me, lax.rem(me + step, n_dev), step - 1)
+        copy.start()
+        sends.append(copy)
     for p in range(parts):
         send(0, me, p, across)
         send(1, me, p, sibling)
     for j, z_ in enumerate(far_z):
         for p in range(parts):
             send(2 + j, me, p, index(z_, y, core))
-    for step in range(1, n_dev):
-        copy = scale_copy(me, lax.rem(me + step, n_dev), step - 1)
-        copy.start()
-        sends.append(copy)
-
-    total = squares(me)
 
     def take_across(k, z_):
         slab = index(z_, 1 - y, core)
         for p in range(parts):
             arrive(slab, p)
             send(k, slab, p, sibling)
-        return squares(slab)
 
     def take_column(k, z_):
         slab = index(z_, y, core)
@@ -120,80 +131,130 @@
             arrive(slab, p)
             send(k, slab, p, across)
             send(k + 1, slab, p, sibling)
-        return squares(slab)
-
-    total += take_across(5, z)
-    total += take_column(6, far_z[0])
-    total += take_column(8, far_z[1])
-    total += take_across(12, far_z[0])
-    total += take_column(10, far_z[2])
-    total += take_across(13, far_z[1])
-    total += take_across(14, far_z[2])
-    for b in range(EARLY, n_slots):
-        table_copy(b).start()
+
+    def take_siblings(z_):
+        for y_ in (y, 1 - y):
+            for p in range(parts):
+                arrive(index(z_, y_, 1 - core), p)
+
+    take_across(5, z)
+    take_column(6, far_z[0])
+    near_copy(EARLY).start()
+    take_column(8, far_z[1])
+    take_across(12, far_z[0])
+    near_copy(EARLY + 1).start()
+    take_column(10, far_z[2])
+    for b in range(EARLY + 2, n_slots):
+        near_copy(b).start()
     for step in range(1, n_dev):
-        scale_copy(lax.rem(me + step, n_dev), me, 0).wait_recv()
-    pad = [scales[d] for d in range(n_dev)] + [jnp.zeros((128 - n_dev, wide), jnp.float32)]
-    scale_cols = jnp.concatenate(pad, axis=0).T
-    for z_ in [z] + far_z:
-        for y_ in (y, 1 - y):
-            slab = index(z_, y_, 1 - core)
-            for p in range(parts):
-                arrive(slab, p)
-            total += squares(slab)
-
+        early_copy(lax.rem(me + step, n_dev), me, 0).wait_recv()
+    total = early[0]
+    for d in range(1, n_dev):
+        total += early[d]
+    total = total[:, :batch]
     inv = lax.rsqrt(total * (1.0 / n_feat) + NORM_EPS)
-    for d in range(n_dev):
-        gain = 1.0 + scale_cols[:d_loc, d:d + 1]
-        normed[d * d_loc:(d + 1) * d_loc, :] = (rows[d].astype(jnp.float32) * inv * gain).astype(jnp.bfloat16)
+    half = n_dev // 2
+    order = [near * half + d for d in range(half)] + [(1 - near) * half + d for d in range(half)]
+    pad = [early[d][:, batch:] for d in order] + [jnp.zeros((128 - n_dev, wide), jnp.float32)]
+    gains = 1.0 + jnp.concatenate(pad, axis=0).T
+    take_siblings(z)
+    take_siblings(far_z[0])
+
+    def normalize(places):
+        for i in places:
+            d = order[i]
+            out = (rows[d].astype(jnp.float32) * inv * gains[:d_loc, i:i + 1]).astype(jnp.bfloat16)
+            normed[pl.ds(pl.multiple_of(d * d_loc, 16), d_loc), :] = out
+
+    normalize(range(half))
+
+    def near_step(b, dst):
+        near_copy(b).wait()
+
+        def body(h, _):
+            at = pl.multiple_of(h * piece, 16)
+            dst[pl.ds(at, piece), :] = jnp.dot(
+                ring[b, pl.ds(at, piece), near_at], normed[near_at, :], preferred_element_type=jnp.float32)
+            return 0
+
+        lax.fori_loop(0, tile // piece, body, 0, unroll=True)
+
+    held = (z0, z1, z2, z3, z4, z5)
+    near_step(0, z0)
+    take_across(13, far_z[1])
+    far_copy(0).start()
+    near_step(1, z1)
+    take_across(14, far_z[2])
+    for b in range(1, n_slots):
+        far_copy(b).start()
+    for b in range(2, n_slots):
+        near_step(b, held[b])
+    take_siblings(far_z[1])
+    take_siblings(far_z[2])
+    normalize(range(half, n_dev))
 
     def dot_piece(b, dst, h):
         at = pl.ds(pl.multiple_of(h * piece, 16), piece)
         dst[at, :] = jnp.dot(ring[lax.rem(b, n_slots), at, :], normed[...], preferred_element_type=jnp.float32)
 
     def epilogue(src, row0, h, carry):
+        ids = [ids_wide[GROUP * k:GROUP * (k + 1), :] for k in range(n_cand)]
+
         def group(g, carry):
             at = h * piece + g * GROUP
             sums, picks = carry[0], list(carry[1:])
             capped = jnp.tanh(src[pl.ds(pl.multiple_of(at, 8), GROUP), :] * (1.0 / SOFT_CAP)) * SOFT_CAP
             capped_ref[pl.ds(pl.multiple_of(row0 + at, 8), GROUP), :] = capped
-            expd = jnp.exp(capped)
-            for q in range(0, GROUP, 8):
-                sums = sums + expd[q:q + 8]
-                token = lax.broadcasted_iota(jnp.int32, (8, batch), 0) + (row0 + at + q)
-                for k in range(n_cand):
-                    picks[k] = jnp.where(token == ids8[8 * k:8 * k + 8, :], capped[q:q + 8], picks[k])
+            sums = sums + jnp.exp(capped)
+            token = lax.broadcasted_iota(jnp.int32, (GROUP, batch), 0) + (row0 + at)
+            picks = [jnp.where(token == i, capped, p) for i, p in zip(ids, picks)]
             return (sums, *picks)
 
         return lax.fori_loop(0, piece // GROUP, group, carry, unroll=True)
 
-    def step(b, dst, src, carry):
+    def far_step(b, dst):
+        far_copy(b).wait()
+
+        def body(h, _):
+            at = pl.multiple_of(h * piece, 16)
+            dst[pl.ds(at, piece), :] += jnp.dot(
+                ring[b, pl.ds(at, piece), far_at], normed[far_at, :], preferred_element_type=jnp.float32)
+            return 0
+
+        lax.fori_loop(0, tile // piece, body, 0, unroll=True)
+        if b + n_slots < n_tiles:
+            table_copy(b + n_slots).start()
+
+    def full_step(b, dst, done, carry):
         table_copy(b).wait()
 
         def body(h, carry):
             dot_piece(b, dst, h)
-            return carry if src is None else epilogue(src, (b - 1) * tile, h, carry)
+            for t in done:
+                carry = epilogue(place(t), t * tile, h, carry)
+            return carry
 
         carry = lax.fori_loop(0, tile // piece, body, carry, unroll=True)
-        @pl.when(b + n_slots < n_tiles)
-        def _():
+        if b + n_slots < n_tiles:
             table_copy(b + n_slots).start()
         return carry
 
-    carry = (jnp.zeros((8, batch), jnp.float32),) * (1 + n_cand)
-    carry = step(0, za, None, carry)
-
-    def pair(i, carry):
-        carry = step(2 * i + 1, zb, za, carry)
-        return step(2 * i + 2, za, zb, carry)
-
-    carry = lax.fori_loop(0, n_tiles // 2 - 1, pair, carry)
-    last = n_tiles - 1
-    carry = step(last, zb, za, carry)
-    carry = lax.fori_loop(0, tile // piece, lambda h, c: epilogue(zb, last * tile, h, c), carry, unroll=True)
+    def place(t):
+        return held[t % len(held)]
+
+    carry = (jnp.zeros((GROUP, batch), jnp.float32),) * (1 + n_cand)
+    for b in range(n_slots):
+        far_step(b, place(b))
+    finished = 0
+    for b in range(n_slots, n_tiles):
+        done = list(range(finished, min(finished + 2, b)))
+        finished += len(done)
+        carry = full_step(b, place(b), done, carry)
+    for t in range(finished, n_tiles):
+        carry = lax.fori_loop(0, tile // piece, lambda h, c, t=t: epilogue(place(t), t * tile, h, c), carry)
 
     mine = [jnp.sum(c, axis=0, keepdims=True) for c in carry]
-    stats[me] = jnp.concatenate(mine + [jnp.zeros((7 - n_cand, batch), jnp.float32)], axis=0)
+    stats[me] = jnp.concatenate(mine, axis=1)
 
     def stat_copy(slab, to, sem):
         return pltpu.make_async_remote_copy(
@@ -213,9 +274,10 @@
     joined = stats[0]
     for d in range(1, n_dev):
         joined += stats[d]
-    lse = jnp.log(joined[0:1, :])
+    lse = jnp.log(joined[:, :batch])
     lse_ref[...] = lse
-    cand_ref[...] = joined[1:1 + n_cand, :] - lse
+    for k in range(n_cand):
+        cand_ref[k:k + 1, :] = joined[:, (k + 1) * batch:(k + 2) * batch] - lse
     for copy in stat_sends:
         copy.wait_send()
 
@@ -275,13 +337,13 @@
             out_specs=[vmem_spec, vmem_spec, vmem_spec],
             scratch_shapes=[
                 pltpu.VMEM((min(SLOTS, vocab // tile), tile, n_feat), jnp.bfloat16),
-                pltpu.VMEM((tile, batch), jnp.float32),
-                pltpu.VMEM((tile, batch), jnp.float32),
+                *[pltpu.VMEM((tile, batch), jnp.float32)] * 6,
                 pltpu.VMEM((n_dev, d_loc, batch), jnp.bfloat16),
-                pltpu.VMEM((n_dev, 1, wide), jnp.float32),
+                pltpu.VMEM((n_dev, 1, batch + wide), jnp.float32),
                 pltpu.VMEM((n_feat, batch), jnp.bfloat16),
-                pltpu.VMEM((8 * n_cand, batch), jnp.int32),
-                pltpu.VMEM((n_dev, 8, batch), jnp.float32),
+                pltpu.VMEM((GROUP * n_cand, batch), jnp.int32),
+                pltpu.VMEM((n_dev, 1, (1 + n_cand) * batch), jnp.float32),
+                dma((min(SLOTS, vocab // tile),)),
                 dma((min(SLOTS, vocab // tile),)),
                 dma((1,)),
                 dma((n_dev, parts)),
@@ -292,7 +354,7 @@
                 dma((n_dev,)),
             ],
             compiler_params=pltpu.CompilerParams(
-                collective_id=0, has_side_effects=True, vmem_limit_bytes=46 * 1024 * 1024),
+                collective_id=0, has_side_effects=True, vmem_limit_bytes=48 * 1024 * 1024),
             cost_estimate=pl.CostEstimate(
                 flops=2 * batch * vocab * n_feat, bytes_accessed=2 * vocab * n_feat, transcendentals=2 * batch * vocab),
             name="stream",

time: 52.3 us -> 50.7 us (0.969)
  Pallas kernels: 50.8 us -> 49.7 us
    pallas_call x1, Pallas kernels: 47.1 us -> 46 us  [device_step(): pl.pallas_call(functools.partial(stream_kernel, n_dev, n_feat), out_shape...]
where the time goes in v4:
time: 50.7 us; the launch traced here: 50.5 us
  Pallas kernels  49.7 us (98%)
  between operations  0.8 us (2%)
    pallas_call x1, Pallas kernels, device_step(): pl.pallas_call(functools.partial(stream_kernel, n_dev, n_feat), out_shape...  46 us
    pallas_call x1, Pallas kernels, device_step(): pl.pallas_call(finish_kernel, out_shape=[jax.ShapeDtypeStruct((batch, voc...  3.65 us

profile of v4, /device:TPU:0, one launch (start us, length us, event | category | flops | bytes accessed | tf_op | source)
XLA Modules:
  0.0 50.5 jit_solution(2516385387059546102)
XLA Ops:
  0.6 46.0 %stream.1 = (f32[16000,256]{1,0:T(8,128)S(1)}, f32[1,256]{1,0:T(1,128)S(1)}, f32[4,256]{1,0:T(4,128)S(1)}) custom-call(bf16[144,256]{1,0:T(8,128)(2,1)} %bitcast.4, bf16[144]{0:T(256)(128)(2,1)} %scale_ref.1, s32[4,256]{1,0:T(4,128)} %bitcast.5, bf16[16000,2304]{1,0:T(8,128)(2,1)} %table_ref.1), custom_call_target="tpu_custom_call" | custom-call | flops 18874368000 | bytes 73728000 | tf_op jit(solution)/shard_map/stream/pallas_call | solution.py:329
  46.7 3.7 %finish.1 = (bf16[256,16000]{1,0:T(8,128)(2,1)}, f32[1,256]{1,0:T(1,128)}, f32[4,256]{1,0:T(4,128)}) custom-call(f32[16000,256]{1,0:T(8,128)S(1)} %get-tuple-element.9.capped_ref, f32[1,256]{1,0:T(1,128)S(1)} %get-tuple-element.10.lse_in, f32[4,256]{1,0:T(4,128)S(1)} %get-tuple-element.11.cand_in), custom_call_target="tpu_custom_call" | custom-call | tf_op jit(solution)/shard_map/finish/pallas_call | solution.py:362

commit v5 on v4

--- a/solution.py
+++ b/solution.py
@@ -143,9 +143,6 @@
     take_column(8, far_z[1])
     take_across(12, far_z[0])
     near_copy(EARLY + 1).start()
-    take_column(10, far_z[2])
-    for b in range(EARLY + 2, n_slots):
-        near_copy(b).start()
     for step in range(1, n_dev):
         early_copy(lax.rem(me + step, n_dev), me, 0).wait_recv()
     total = early[0]
@@ -180,14 +177,19 @@
         lax.fori_loop(0, tile // piece, body, 0, unroll=True)
 
     held = (z0, z1, z2, z3, z4, z5)
-    near_step(0, z0)
+    near_step(0, held[0])
+    take_column(10, far_z[2])
+    for b in range(EARLY + 2, n_slots):
+        near_copy(b).start()
+    far_copy(0).start()
+    near_step(1, held[1])
     take_across(13, far_z[1])
-    far_copy(0).start()
-    near_step(1, z1)
+    far_copy(1).start()
+    near_step(2, held[2])
     take_across(14, far_z[2])
-    for b in range(1, n_slots):
+    for b in range(2, n_slots):
         far_copy(b).start()
-    for b in range(2, n_slots):
+    for b in range(3, n_slots):
         near_step(b, held[b])
     take_siblings(far_z[1])
     take_siblings(far_z[2])

time: 50.7 us -> 50.3 us (level)
  no operation moved by 1% of the time
where the time goes in v5:
time: 50.3 us; the launch traced here: 50.1 us
  Pallas kernels  49.3 us (98%)
  between operations  0.8 us (2%)
    pallas_call x1, Pallas kernels, device_step(): pl.pallas_call(functools.partial(stream_kernel, n_dev, n_feat), out_shape...  45.7 us
    pallas_call x1, Pallas kernels, device_step(): pl.pallas_call(finish_kernel, out_shape=[jax.ShapeDtypeStruct((batch, voc...  3.65 us

profile of v5, /device:TPU:0, one launch (start us, length us, event | category | flops | bytes accessed | tf_op | source)
XLA Modules:
  0.0 50.1 jit_solution(1375260664608501139)
XLA Ops:
  0.6 45.7 %stream.1 = (f32[16000,256]{1,0:T(8,128)S(1)}, f32[1,256]{1,0:T(1,128)S(1)}, f32[4,256]{1,0:T(4,128)S(1)}) custom-call(bf16[144,256]{1,0:T(8,128)(2,1)} %bitcast.4, bf16[144]{0:T(256)(128)(2,1)} %scale_ref.1, s32[4,256]{1,0:T(4,128)} %bitcast.5, bf16[16000,2304]{1,0:T(8,128)(2,1)} %table_ref.1), custom_call_target="tpu_custom_call" | custom-call | flops 18874368000 | bytes 73728000 | tf_op jit(solution)/shard_map/stream/pallas_call | solution.py:331
  46.3 3.7 %finish.1 = (bf16[256,16000]{1,0:T(8,128)(2,1)}, f32[1,256]{1,0:T(1,128)}, f32[4,256]{1,0:T(4,128)}) custom-call(f32[16000,256]{1,0:T(8,128)S(1)} %get-tuple-element.9.capped_ref, f32[1,256]{1,0:T(1,128)S(1)} %get-tuple-element.10.lse_in, f32[4,256]{1,0:T(4,128)S(1)} %get-tuple-element.11.cand_in), custom_call_target="tpu_custom_call" | custom-call | tf_op jit(solution)/shard_map/finish/pallas_call | solution.py:364
